TPU v7x, 32 devices: a whole 2x2x4 slice. The times are simulated.
32 devices in a mesh: island: 2 (over x), own: 16 (over z, y, core).
Axes of the slice: x: 2, y: 2, z: 4, core: 2. Of those that a mesh axis runs over, the one named last changes fastest.
Arguments:
- master: float32 [8, 2048, 8192], P(None, ('island', 'own')), may hold values from -6 to 6
- momentum: float32 [8, 2048, 8192], P(None, ('island', 'own')), may hold values from -6 to 6
- deltas: float32 [2, 2048, 8192], P('island', None, 'own'), may hold values from -6 to 6
- old_path: int32 [2], replicated, may hold values from 0 to 255
- new_path: int32 [2], replicated, may hold values from 0 to 255
- path_module: int32 [256], replicated, may hold values from 0 to 7
- island_steps: int32 [2], replicated, may hold values from 1 to 9
Outputs:
- new_master: float32 [8, 2048, 8192], P(None, ('island', 'own'))
- new_momentum: float32 [8, 2048, 8192], P(None, ('island', 'own'))
- new_module: float32 [2, 2048, 8192], P('island', None, 'own')
All inputs are finite; a program needn't handle non-finite values.
Results may differ from a plain program's by a relative error of at most 0.00007.
Values sent between devices are 32-bit elements; how exact they have to be, the bound alone decides.
A program may use at most 192 MiB of HBM per device.

v0:
```python
import jax
import jax.numpy as jnp
from jax import lax
from jax.sharding import PartitionSpec as P


def shards(master, momentum, deltas, old_path, new_path, path_module, island_steps):
    modules = master.shape[0]
    received = lax.all_to_all(
        lax.all_to_all(deltas, "island", split_axis=1, concat_axis=0, tiled=True),
        "own",
        split_axis=1,
        concat_axis=2,
        tiled=True,
    )
    old_module = path_module[old_path]
    chosen = old_module[None, :] == jnp.arange(modules, dtype=jnp.int32)[:, None]
    mixing = chosen.astype(jnp.float32) * island_steps.astype(jnp.float32)[None, :]
    divisor = jnp.maximum(jnp.sum(mixing, axis=1), 1.0)
    average = jnp.einsum("kj,jrc->krc", mixing, received, precision=lax.Precision.HIGHEST)
    average = average / divisor[:, None, None]
    new_momentum = 0.9 * momentum + average
    new_master = master - 0.7 * (average + 0.9 * new_momentum)
    new_index = path_module[new_path]
    picked = jnp.take(new_master, new_index, axis=0)
    by_island = lax.all_to_all(picked, "island", split_axis=0, concat_axis=1, tiled=True)
    spread = lax.all_to_all(by_island, "own", split_axis=2, concat_axis=1, tiled=True)
    owners = lax.axis_size("own")
    isles = lax.axis_size("island")
    rows_block = picked.shape[1]
    width = spread.shape[2]
    reshaped = spread.reshape(1, owners, isles, rows_block, width)
    new_module = jnp.transpose(reshaped, (0, 2, 1, 3, 4)).reshape(
        1, owners * isles * rows_block, width
    )
    return (new_master, new_momentum, new_module)


def solution(mesh):
    return jax.shard_map(
        shards,
        mesh=mesh,
        in_specs=(
            P(None, ("island", "own"), None),
            P(None, ("island", "own"), None),
            P("island", None, "own"),
            P(),
            P(),
            P(),
            P(),
        ),
        out_specs=(
            P(None, ("island", "own"), None),
            P(None, ("island", "own"), None),
            P("island", None, "own"),
        ),
        check_vma=False,
    )
```

profile of v0, /device:TPU:13, one launch (start us, length us, event | category | flops | bytes accessed | tf_op | source)
XLA Modules:
  0.0 422.7 jit_solution(4052904943717880893)
XLA Ops:
  0.6 0.0 copy-start
  0.6 7.0 %copy.40 = f32[1,2048,512]{2,0,1:T(1,128)S(1)} copy(f32[1,2048,512]{2,1,0:T(8,128)} %param.9) | data formatting | bytes 8388608 | tf_op args[2]
  7.7 49.5 %all_to_all.57 = f32[1,2048,512]{2,0,1:T(1,128)S(1)} all-to-all(f32[1,2048,512]{2,0,1:T(1,128)S(1)} %copy.40), channel_id=1, replica_groups=mesh['island'=2,'own'=16] {'island'}, dimensions={1} | all-to-all | bytes 8388608 | tf_op jit(solution)/shard_map/all_to_all | solution.py:10
  57.1 0.4 copy.52
  57.6 5.2 %copy.41 = f32[2,1024,512]{2,0,1:T(2,128)} copy(f32[2,1024,512]{2,1,0:T(8,128)S(1)} %bitcast.29) | data formatting | bytes 8388608 | tf_op jit(solution)/shard_map/all_to_all | solution.py:10
  62.8 0.0 copy-start.2
  62.8 0.0 copy-start.4
  62.8 7.5 %all-to-all-start.1 = ((f32[2,1024,512]{2,0,1:T(2,128)}), f32[2,1024,512]{2,0,1:T(2,128)}, u32[]{:S(2)}, u32[]{:S(2)}) async-start(f32[2,1024,512]{2,0,1:T(2,128)} %copy.41), calls=%async_computation.1 | async-start | bytes 8388608 | tf_op jit(solution)/shard_map/all_to_all | solution.py:9
  70.4 0.0 copy-done.2
  70.4 0.0 copy-done.3
  70.4 0.0 copy-done
  70.4 0.6 gather_fusion
  71.1 0.0 copy-done.4
  71.1 0.6 gather_fusion.1
  71.7 0.1 fusion.2
  71.8 91.0 %all-to-all-done.1 = f32[2,1024,512]{2,0,1:T(2,128)} async-done(((f32[2,1024,512]{2,0,1:T(2,128)}), f32[2,1024,512]{2,0,1:T(2,128)}, u32[]{:S(2)}, u32[]{:S(2)}) %all-to-all-start.1) | async-done | bytes 4194336 | tf_op jit(solution)/shard_map/all_to_all | solution.py:9
  162.8 3.0 copy.42
  165.8 4.4 %copy.43 = f32[2,64,16,512]{3,2,0,1:T(8,128)} copy(f32[2,64,16,512]{3,1,2,0:T(8,128)S(1)} %bitcast.30) | data formatting | bytes 8388608 | tf_op jit(solution)/shard_map/all_to_all | solution.py:9
  170.3 6.6 %all_to_all.47 = f32[2,64,8192]{2,0,1:T(2,128)} reshape(f32[2,64,16,512]{3,2,0,1:T(8,128)} %copy.43) | data formatting | bytes 8388608 | tf_op jit(solution)/shard_map/all_to_all | solution.py:9
  176.8 50.4 %fusion = (f32[8,64,8192]{2,0,1:T(8,128)}, f32[8,64,8192]{2,0,1:T(8,128)S(1)}) fusion(f32[8,64,8192]{2,1,0:T(8,128)} %param.8, f32[8,64,8192]{2,1,0:T(8,128)} %param.7, f32[8]{0:T(128)S(1)} %broadcast_maximum_fusion, f32[2,64,8192]{2,0,1:T(2,128)} %all_to_all.47, f32[2]{0:T(128)S(1)} %convert_element_type.4, s32[2]{0:T(128)S(1)} %gather_fusion), kind=kOutput, calls=%fused_computation.5 | convolution fusion | flops 130023456 | bytes 71303216 | tf_op jit(solution)/shard_map/kj,jrc->krc/dot_general | solution.py:20
  227.3 15.1 %copy.50 = f32[8,64,8192]{2,1,0:T(8,128)} copy(f32[8,64,8192]{2,0,1:T(8,128)S(1)} %get-tuple-element.19) | data formatting | bytes 33554432
  242.3 8.6 %gather_fusion.2 = f32[2,64,8192]{2,1,0:T(8,128)} fusion(f32[8,64,8192]{2,1,0:T(8,128)} %copy.50, s32[1024]{0:T(1024)S(1)} %pad_clamp_fusion), kind=kCustom, calls=%fused_computation.2 | custom fusion | bytes 8388616 | tf_op jit(solution)/shard_map/jit(_take)/gather | solution.py:25
  250.9 2.7 broadcast_select_fusion
  253.6 51.1 %all_to_all.58 = f32[2,64,8192]{2,1,0:T(8,128)} all-to-all(f32[2,64,8192]{2,1,0:T(8,128)S(1)} %broadcast_select_fusion), channel_id=1, replica_groups=mesh['island'=2,'own'=16] {'island'}, dimensions={0} | all-to-all | bytes 8388608 | tf_op jit(solution)/shard_map/all_to_all | solution.py:26
  304.7 9.6 %copy.47 = f32[1,128,8192]{1,0,2:T(1,128)} copy(f32[1,128,8192]{2,1,0:T(8,128)} %bitcast.31) | data formatting | bytes 8388608 | tf_op jit(solution)/shard_map/all_to_all | solution.py:26
  314.3 5.6 %all-to-all-start.3 = ((f32[1,128,8192]{1,0,2:T(1,128)}), f32[1,128,8192]{1,0,2:T(1,128)}, u32[]{:S(2)}, u32[]{:S(2)}) async-start(f32[1,128,8192]{1,0,2:T(1,128)} %copy.47), calls=%async_computation.3 | async-start | bytes 8388608 | tf_op jit(solution)/shard_map/all_to_all | solution.py:27
  319.9 17.8 %copy.51 = f32[8,64,8192]{2,1,0:T(8,128)} copy(f32[8,64,8192]{2,0,1:T(8,128)} %get-tuple-element.18) | data formatting | bytes 33554432
  337.7 74.7 %all-to-all-done.3 = f32[1,128,8192]{1,0,2:T(1,128)} async-done(((f32[1,128,8192]{1,0,2:T(1,128)}), f32[1,128,8192]{1,0,2:T(1,128)}, u32[]{:S(2)}, u32[]{:S(2)}) %all-to-all-start.3) | async-done | bytes 4194336 | tf_op jit(solution)/shard_map/all_to_all | solution.py:27
  412.4 5.4 %copy.48 = f32[1,16,128,512]{3,2,1,0:T(8,128)} copy(f32[1,16,128,512]{2,3,1,0:T(8,128)} %bitcast.7) | data formatting | bytes 8388608 | tf_op jit(solution)/shard_map/all_to_all | solution.py:27
  417.7 0.0 copy-start.1
  417.7 4.9 %copy.49 = f32[1,2,16,64,512]{4,3,2,1,0:T(8,128)} copy(f32[1,2,16,64,512]{4,3,1,2,0:T(8,128)} %bitcast.32) | data formatting | bytes 8388608 | tf_op jit(solution)/shard_map/transpose | solution.py:33
  422.7 0.0 copy-done.1
  (10 shorter events, 0.1 us)
Async XLA Ops:
  0.6 69.8 %copy-start = (s32[256]{0:T(256)S(1)}, s32[256]{0:T(256)}, u32[]{:S(2)}) copy-start(s32[256]{0:T(256)} %param.12) | copy-start | bytes 3076
  62.8 7.5 %copy-start.2 = (s32[2]{0:T(128)S(1)}, s32[2]{0:T(128)}, u32[]{:S(2)}) copy-start(s32[2]{0:T(128)} %param.13) | copy-start | bytes 28
  62.8 7.5 %copy-start.3 = (s32[2]{0:T(128)S(1)}, s32[2]{0:T(128)}, u32[]{:S(2)}) copy-start(s32[2]{0:T(128)} %param.10) | copy-start | bytes 28
  62.8 8.2 %copy-start.4 = (s32[2]{0:T(128)S(1)}, s32[2]{0:T(128)}, u32[]{:S(2)}) copy-start(s32[2]{0:T(128)} %param.11) | copy-start | bytes 28
  62.8 100.0 %all-to-all-start.1 = ((f32[2,1024,512]{2,0,1:T(2,128)}), f32[2,1024,512]{2,0,1:T(2,128)}, u32[]{:S(2)}, u32[]{:S(2)}) async-start(f32[2,1024,512]{2,0,1:T(2,128)} %copy.41), calls=%async_computation.1 | async-start | bytes 8388608 | tf_op jit(solution)/shard_map/all_to_all | solution.py:9
  314.3 98.1 %all-to-all-start.3 = ((f32[1,128,8192]{1,0,2:T(1,128)}), f32[1,128,8192]{1,0,2:T(1,128)}, u32[]{:S(2)}, u32[]{:S(2)}) async-start(f32[1,128,8192]{1,0,2:T(1,128)} %copy.47), calls=%async_computation.3 | async-start | bytes 8388608 | tf_op jit(solution)/shard_map/all_to_all | solution.py:27
  417.7 4.9 %copy-start.1 = (s32[256]{0:T(256)S(1)}, s32[256]{0:T(256)}, u32[]{:S(2)}) copy-start(s32[256]{0:T(256)} %param.12) | copy-start | bytes 3076
where the time goes:
time: 424 us; the launch traced here: 423 us
  waiting for transfers between devices  166 us (39%)
  blocking collectives  101 us (24%)
  local copies, waits for them, and re-layouts  89.4 us (21%)
  matrix products  50.4 us (12%)
  starting transfers between devices  13.1 us (3%)
    all_to_all x1, waiting for transfers between devices, shards(): lax.all_to_all(lax.all_to_all(deltas, 'island', split_axis=1, concat_axis...  91 us
    all_to_all x1, waiting for transfers between devices, shards(): lax.all_to_all(by_island, 'own', split_axis=2, concat_axis=1, tiled=True)  74.7 us
    all_to_all x1, blocking collectives, shards(): lax.all_to_all(picked, 'island', split_axis=0, concat_axis=1, tiled=True)  51.1 us
    dot_general x1, matrix products, shards(): jnp.einsum('kj,jrc->krc', mixing, received, precision=lax.Precision.HIGHEST)  50.4 us
    all_to_all x1, blocking collectives, shards(): lax.all_to_all(deltas, 'island', split_axis=1, concat_axis=0, tiled=True)  49.5 us
    unnamed x14, local copies, waits for them, and re-layouts  40.3 us
    all_to_all x3, local copies, waits for them, and re-layouts, shards(): lax.all_to_all(lax.all_to_all(deltas, 'island', split_axis=1, concat_axis...  14 us
    all_to_all x1, local copies, waits for them, and re-layouts, shards(): lax.all_to_all(picked, 'island', split_axis=0, concat_axis=1, tiled=True)  9.63 us
  transfers between devices with their start and end apart: 2, of which 2 were waited for; matrix products, arithmetic and copies ran while one was open for 5% of the time, Pallas kernels for 0%

commit v1 on v0

v1 whole, which is shorter than its diff:
```python
import functools

import jax
import jax.numpy as jnp
from jax import lax
from jax.experimental import pallas as pl
from jax.experimental.pallas import tpu as pltpu
from jax.sharding import PartitionSpec as P


def mix(weight_ref, k, received, isles):
    total = weight_ref[k, 0] * received[0]
    for j in range(1, isles):
        total = total + weight_ref[k, j] * received[j]
    return total


def step(master, momentum, average):
    new_momentum = 0.9 * momentum + average
    return master - 0.7 * (average + 0.9 * new_momentum), new_momentum


def pick_kernel(isles, per, width, index_ref, weight_ref, master_ref, momentum_ref, received_ref, out_ref):
    k = index_ref[pl.program_id(0)]
    for p in range(per):
        columns = slice(p * width, (p + 1) * width)
        average = mix(weight_ref, k, [received_ref[j, p] for j in range(isles)], isles)
        out_ref[0, p] = step(master_ref[0, :, columns], momentum_ref[0, :, columns], average)[0]


def update_kernel(isles, modules, per, width, weight_ref, master_ref, momentum_ref, received_ref, new_master_ref, new_momentum_ref):
    for p in range(per):
        columns = slice(p * width, (p + 1) * width)
        received = [received_ref[j, p] for j in range(isles)]
        for k in range(modules):
            average = mix(weight_ref, k, received, isles)
            new_master, new_momentum = step(master_ref[k, :, columns], momentum_ref[k, :, columns], average)
            new_master_ref[k, :, columns] = new_master
            new_momentum_ref[k, :, columns] = new_momentum


def divisor_below(count, bound):
    return max(d for d in range(1, count + 1) if count % d == 0 and d <= max(bound, 1))


def pick(master, momentum, received, index, weight):
    modules, rows, _ = master.shape
    isles, owners, _, width = received.shape
    per = divisor_below(owners, (1 << 20) // (rows * width * 4))
    return pl.pallas_call(
        functools.partial(pick_kernel, isles, per, width),
        grid_spec=pltpu.PrefetchScalarGridSpec(
            num_scalar_prefetch=2,
            grid=(isles, owners // per),
            in_specs=[
                pl.BlockSpec((1, rows, per * width), lambda j, c, index, weight: (index[j], 0, c)),
                pl.BlockSpec((1, rows, per * width), lambda j, c, index, weight: (index[j], 0, c)),
                pl.BlockSpec((isles, per, rows, width), lambda j, c, index, weight: (0, c, 0, 0)),
            ],
            out_specs=pl.BlockSpec((1, per, rows, width), lambda j, c, index, weight: (j, c, 0, 0)),
        ),
        out_shape=jax.ShapeDtypeStruct((isles, owners, rows, width), jnp.float32),
        compiler_params=pltpu.CompilerParams(vmem_limit_bytes=32 << 20),
        cost_estimate=pl.CostEstimate(flops=8 * received.size, bytes_accessed=4 * 5 * received.size, transcendentals=0),
        name="pick",
    )(index, weight, master, momentum, received)


def update(master, momentum, received, weight):
    modules, rows, columns = master.shape
    isles, owners, _, width = received.shape
    per = divisor_below(owners, (2 << 20) // (modules * rows * width * 4))
    big = pl.BlockSpec((modules, rows, per * width), lambda c, weight: (0, 0, c))
    return pl.pallas_call(
        functools.partial(update_kernel, isles, modules, per, width),
        grid_spec=pltpu.PrefetchScalarGridSpec(
            num_scalar_prefetch=1,
            grid=(owners // per,),
            in_specs=[big, big, pl.BlockSpec((isles, per, rows, width), lambda c, weight: (0, c, 0, 0))],
            out_specs=[big, big],
        ),
        out_shape=[jax.ShapeDtypeStruct(master.shape, jnp.float32)] * 2,
        compiler_params=pltpu.CompilerParams(vmem_limit_bytes=40 << 20),
        cost_estimate=pl.CostEstimate(flops=8 * master.size, bytes_accessed=4 * 4 * master.size + 4 * received.size, transcendentals=0),
        name="update",
    )(weight, master, momentum, received)


def shards(master, momentum, deltas, old_path, new_path, path_module, island_steps):
    modules, rows, _ = master.shape
    owners = lax.axis_size("own")
    isles = lax.axis_size("island")
    width = deltas.shape[2]
    old_module = path_module[old_path]
    chosen = old_module[None, :] == jnp.arange(modules, dtype=jnp.int32)[:, None]
    mixing = chosen.astype(jnp.float32) * island_steps.astype(jnp.float32)[None, :]
    divisor = jnp.maximum(jnp.sum(mixing, axis=1), 1.0)
    weight = mixing / divisor[:, None]
    index = path_module[new_path]

    blocks = deltas.reshape(isles * owners, rows, width)
    received = lax.all_to_all(blocks, ("island", "own"), split_axis=0, concat_axis=0, tiled=True)
    received = received.reshape(isles, owners, rows, width)
    picked = pick(master, momentum, received, index, weight)
    spread = lax.all_to_all(
        picked.reshape(isles * owners, rows, width), ("island", "own"), split_axis=0, concat_axis=0, tiled=True
    )
    new_master, new_momentum = update(master, momentum, received, weight)
    return (new_master, new_momentum, spread.reshape(deltas.shape))


def solution(mesh):
    return jax.shard_map(
        shards,
        mesh=mesh,
        in_specs=(
            P(None, ("island", "own"), None),
            P(None, ("island", "own"), None),
            P("island", None, "own"),
            P(),
            P(),
            P(),
            P(),
        ),
        out_specs=(
            P(None, ("island", "own"), None),
            P(None, ("island", "own"), None),
            P("island", None, "own"),
        ),
        check_vma=False,
    )
```

time: 424 us -> 215 us (0.51)
  the two profiles are of different devices: /device:TPU:13 before, /device:TPU:0 now
where the time goes in v1:
time: 215 us
  waiting for transfers between devices  163 us (76%)
  Pallas kernels  32.1 us (15%)
  starting transfers between devices  11 us (5%)
  local copies, waits for them, and re-layouts  7.97 us (4%)
    all_to_all x1, waiting for transfers between devices, shards(): lax.all_to_all(blocks, ('island', 'own'), split_axis=0, concat_axis=0, ti...  93.2 us
    all_to_all x1, waiting for transfers between devices, shards(): lax.all_to_all(picked.reshape(isles * owners, rows, width), ('island', 'o...  69.9 us
    pallas_call x1, Pallas kernels, update(): pl.pallas_call(functools.partial(update_kernel, isles, modules, per, widt...  24.9 us
    all_to_all x1, starting transfers between devices, shards(): lax.all_to_all(blocks, ('island', 'own'), split_axis=0, concat_axis=0, ti...  7.46 us
    pallas_call x1, Pallas kernels, pick(): pl.pallas_call(functools.partial(pick_kernel, isles, per, width), grid_sp...  7.26 us
    unnamed x13, local copies, waits for them, and re-layouts  6.69 us
  transfers between devices with their start and end apart: 2, of which 2 were waited for; matrix products, arithmetic and copies ran while one was open for 1% of the time, Pallas kernels for 12%

profile of v1, /device:TPU:0, one launch (start us, length us, event | category | flops | bytes accessed | tf_op | source)
XLA Modules:
  0.0 215.2 jit_solution(11346792949743937808)
XLA Ops:
  0.6 0.0 copy-start
  0.6 0.0 copy-start.3
  0.7 0.0 copy-start.4
  0.7 0.0 copy-start.5
  0.7 7.5 %all-to-all-start = ((f32[32,64,512]{2,1,0:T(8,128)}), f32[32,64,512]{2,1,0:T(8,128)}, u32[]{:S(2)}, u32[]{:S(2)}) async-start(f32[32,64,512]{2,1,0:T(8,128)} %bitcast.5), calls=%async_computation | async-start | bytes 8388608 | tf_op jit(solution)/shard_map/all_to_all | solution.py:102
  8.1 0.0 copy-done.3
  8.2 0.0 copy-done.4
  8.2 0.0 copy-done
  8.2 0.6 gather_fusion.1
  8.9 0.0 copy-done.5
  8.9 0.6 gather_fusion
  9.5 0.1 select_reduce_fusion
  9.6 0.1 select_divide_fusion.weight_ref
  9.7 93.2 %all-to-all-done = f32[32,64,512]{2,1,0:T(8,128)} async-done(((f32[32,64,512]{2,1,0:T(8,128)}), f32[32,64,512]{2,1,0:T(8,128)}, u32[]{:S(2)}, u32[]{:S(2)}) %all-to-all-start) | async-done | bytes 4194336 | tf_op jit(solution)/shard_map/all_to_all | solution.py:102
  102.9 7.3 %pick.1 = f32[2,16,64,512]{3,2,1,0:T(8,128)S(1)} custom-call(s32[2]{0:T(128)S(1)} %gather_fusion.1, f32[8,2]{1,0:T(8,128)S(1)} %select_divide_fusion.weight_ref, f32[8,64,8192]{2,1,0:T(8,128)} %master_ref.3, f32[8,64,8192]{2,1,0:T(8,128)} %momentum_ref.3, f32[2,16,64,512]{3,2,1,0:T(8,128)} %bitcast.1.received_ref), custom_call_target="tpu_custom_call" | custom-call | flops 8388608 | bytes 20971520 | tf_op jit(solution)/shard_map/pick/pallas_call | solution.py:50
  110.1 0.0 copy-start.2
  110.2 2.0 copy-done.2
  112.2 3.6 %all-to-all-start.1 = ((f32[32,64,512]{2,1,0:T(8,128)}), f32[32,64,512]{2,1,0:T(8,128)}, u32[]{:S(2)}, u32[]{:S(2)}) async-start(f32[32,64,512]{2,1,0:T(8,128)} %bitcast.4), calls=%async_computation.1 | async-start | bytes 8388608 | tf_op jit(solution)/shard_map/all_to_all | solution.py:105
  115.7 24.9 %update.1 = (f32[8,64,8192]{2,1,0:T(8,128)}, f32[8,64,8192]{2,1,0:T(8,128)}) custom-call(f32[8,2]{1,0:T(8,128)S(1)} %select_divide_fusion.weight_ref, f32[8,64,8192]{2,1,0:T(8,128)} %master_ref.3, f32[8,64,8192]{2,1,0:T(8,128)} %momentum_ref.3, f32[2,16,64,512]{3,2,1,0:T(8,128)} %bitcast.1.received_ref), custom_call_target="tpu_custom_call" | custom-call | flops 33554432 | bytes 71303168 | tf_op jit(solution)/shard_map/update/pallas_call | solution.py:74
  140.6 69.9 %all-to-all-done.1 = f32[32,64,512]{2,1,0:T(8,128)} async-done(((f32[32,64,512]{2,1,0:T(8,128)}), f32[32,64,512]{2,1,0:T(8,128)}, u32[]{:S(2)}, u32[]{:S(2)}) %all-to-all-start.1) | async-done | bytes 4194336 | tf_op jit(solution)/shard_map/all_to_all | solution.py:105
  210.5 0.0 copy-start.1
  210.5 4.7 %copy.11 = f32[1,2048,512]{2,1,0:T(8,128)} copy(f32[1,2048,512]{2,1,0:T(8,128)} %bitcast.3) | data formatting | bytes 8388608
  215.2 0.0 copy-done.1
  (6 shorter events, 0.0 us)
Async XLA Ops:
  0.6 7.6 %copy-start = (s32[256]{0:T(256)S(1)}, s32[256]{0:T(256)}, u32[]{:S(2)}) copy-start(s32[256]{0:T(256)} %param.12) | copy-start | bytes 3076
  0.6 7.5 %copy-start.3 = (s32[2]{0:T(128)S(1)}, s32[2]{0:T(128)}, u32[]{:S(2)}) copy-start(s32[2]{0:T(128)} %param.13) | copy-start | bytes 28
  0.7 7.5 %copy-start.4 = (s32[2]{0:T(128)S(1)}, s32[2]{0:T(128)}, u32[]{:S(2)}) copy-start(s32[2]{0:T(128)} %param.11) | copy-start | bytes 28
  0.7 8.2 %copy-start.5 = (s32[2]{0:T(128)S(1)}, s32[2]{0:T(128)}, u32[]{:S(2)}) copy-start(s32[2]{0:T(128)} %param.10) | copy-start | bytes 28
  0.7 102.2 %all-to-all-start = ((f32[32,64,512]{2,1,0:T(8,128)}), f32[32,64,512]{2,1,0:T(8,128)}, u32[]{:S(2)}, u32[]{:S(2)}) async-start(f32[32,64,512]{2,1,0:T(8,128)} %bitcast.5), calls=%async_computation | async-start | bytes 8388608 | tf_op jit(solution)/shard_map/all_to_all | solution.py:102
  110.1 2.0 copy-start.2
  112.2 98.4 %all-to-all-start.1 = ((f32[32,64,512]{2,1,0:T(8,128)}), f32[32,64,512]{2,1,0:T(8,128)}, u32[]{:S(2)}, u32[]{:S(2)}) async-start(f32[32,64,512]{2,1,0:T(8,128)} %bitcast.4), calls=%async_computation.1 | async-start | bytes 8388608 | tf_op jit(solution)/shard_map/all_to_all | solution.py:105
  210.5 4.7 %copy-start.1 = (s32[256]{0:T(256)S(1)}, s32[256]{0:T(256)}, u32[]{:S(2)}) copy-start(s32[256]{0:T(256)} %param.12) | copy-start | bytes 3076
